TPU v7x, 32 devices: a whole 2x2x4 slice. The times are simulated.
32 devices in a mesh: dp: 8 (over z, x), feat: 4 (over y, core).
Axes of the slice: x: 2, y: 2, z: 4, core: 2. Of those that a mesh axis runs over, the one named last changes fastest.
Arguments:
- features: float32 [24576, 2048], P('dp', 'feat'), may hold values from -200 to 200
- gamma: float32 [2048], P('feat'), may hold values from 0.5 to 1.5
- beta: float32 [2048], P('feat'), may hold values from -3 to 3
- weight: bfloat16 [2048, 2048], P(None, 'feat'), may hold values from -0.125 to 0.125
- bias: float32 [2048], P('feat'), may hold values from -3 to 3
Outputs:
- activated: float32 [24576, 2048], P('dp', 'feat')
All inputs are finite; a program needn't handle non-finite values.
Results may differ from a plain program's by a relative error of at most 0.0026.
Values may be sent and summed in bfloat16 or wider, within the bound.
No kernel may reach another device: no remote copies, remote signals or barrier semaphores. Data moves between devices by JAX's collectives and lax.ppermute only.
A program may use at most 128 MiB of HBM per device.

v0:
```python
import jax
import jax.numpy as jnp
from jax import lax
from jax.sharding import PartitionSpec as P


def local(features, gamma, beta, weight, bias):
    rows = features.shape[0]
    total_rows = rows * lax.axis_size("dp")
    sums = lax.psum(jnp.sum(features, axis=0), "dp")
    mean = sums / total_rows
    centred_here = features - mean
    devs = lax.psum(jnp.sum(centred_here * centred_here, axis=0), "dp")
    var = devs / total_rows
    scale = gamma / jnp.sqrt(var + 1e-05)
    normed = ((features - mean) * scale + beta).astype(jnp.bfloat16)
    product = jnp.dot(
        lax.all_gather(normed, "feat", axis=1, tiled=True),
        weight,
        preferred_element_type=jnp.float32,
    )
    return jnp.maximum(product + bias, 0.0)


def solution(mesh):
    placed = (P("dp", "feat"), P("feat"), P("feat"), P(None, "feat"), P("feat"))
    return jax.shard_map(
        local, mesh=mesh, in_specs=placed, out_specs=P("dp", "feat"), check_vma=False
    )
```

profile of v0, /device:TPU:0, one launch (start us, length us, event | category | flops | bytes accessed | tf_op | source)
XLA Modules:
  0.0 158.3 jit_solution(14574581504709749969)
XLA Ops:
  6.5 0.0 copy-start
  6.5 0.0 copy-start.2
  6.5 0.0 copy-start.1
  6.5 0.0 all-gather.2.cloned.1.call-start
  6.5 3.4 %reduce_sum.18 = f32[512]{0:T(512)S(1)} reduce(f32[3072,512]{1,0:T(8,128)} %param.5, f32[]{:T(128)} %constant.3.clone.1), dimensions={0}, to_apply=%region_0.0 | reduce | flops 1572352 | bytes 6293508 | tf_op jit(solution)/shard_map/reduce_sum | solution.py:10
  9.9 23.1 %psum.14 = f32[512]{0:T(512)S(1)} all-reduce(f32[512]{0:T(512)S(1)} %reduce_sum.18), channel_id=1, replica_groups=mesh['dp'=8,'feat'=4] {'dp'}, use_global_device_ids=true, to_apply=%region_1.0 | all-reduce | flops 512 | bytes 4096 | tf_op jit(solution)/shard_map/psum | solution.py:10
  33.1 3.5 %multiply_reduce_fusion = f32[512]{0:T(512)S(1)} fusion(f32[3072,512]{1,0:T(8,128)} %param.5, f32[512]{0:T(512)S(1)} %broadcast_multiply_fusion), kind=kLoop, calls=%fused_computation.2 | loop fusion | flops 4718080 | bytes 6295552 | tf_op jit(solution)/shard_map/reduce_sum | solution.py:13
  36.6 17.1 %psum.15 = f32[512]{0:T(512)S(1)} all-reduce(f32[512]{0:T(512)S(1)} %multiply_reduce_fusion), channel_id=1, replica_groups=mesh['dp'=8,'feat'=4] {'dp'}, use_global_device_ids=true, to_apply=%region_3.0 | all-reduce | flops 512 | bytes 4096 | tf_op jit(solution)/shard_map/psum | solution.py:13
  53.7 0.0 copy-done.2
  53.7 0.0 copy-done.1
  53.7 0.0 copy-start.3
  53.7 5.4 %add_convert_fusion = bf16[3072,512]{1,0:T(8,128)(2,1)} fusion(f32[3072,512]{1,0:T(8,128)} %param.5, f32[512]{0:T(512)S(1)} %copy-done.1, f32[512]{0:T(512)S(1)} %rsqrt_multiply_fusion, f32[512]{0:T(512)S(1)} %broadcast_multiply_fusion), kind=kLoop, calls=%fused_computation.1 | loop fusion | flops 6291456 | bytes 9443328 | tf_op jit(solution)/shard_map/convert_element_type | solution.py:16
  59.1 0.0 all-gather.2.cloned.1.call-update
  59.1 81.0 %all-gather.2.cloned.1.call-done = bf16[3072,2048]{1,0:T(8,128)(2,1)} async-done(((bf16[3072,512]{1,0:T(8,128)(2,1)}), bf16[3072,2048]{1,0:T(8,128)(2,1)}) %all-gather.2.cloned.1.call-update) | async-done | bytes 12582928 | tf_op jit(solution)/shard_map/all_gather | solution.py:18
  140.1 0.0 copy-done
  140.1 0.0 copy-done.3
  140.1 11.3 %add_maximum_fusion = f32[3072,512]{1,0:T(8,128)} fusion(bf16[3072,2048]{1,0:T(8,128)(2,1)} %all-gather.2.cloned.1.call-done, bf16[2048,512]{1,0:T(8,128)(2,1)S(1)} %copy-done, f32[512]{0:T(512)S(1)} %copy-done.3), kind=kOutput, calls=%fused_computation | convolution fusion | flops 6445596672 | bytes 20973568 | tf_op jit(solution)/shard_map/dot_general | solution.py:17
  (2 shorter events, 0.0 us)
Async XLA Ops:
  6.5 133.6 %copy-start = (bf16[2048,512]{1,0:T(8,128)(2,1)S(1)}, bf16[2048,512]{1,0:T(8,128)(2,1)}, u32[]{:S(2)}) copy-start(bf16[2048,512]{1,0:T(8,128)(2,1)} %param.8) | copy-start | bytes 6291460
  6.5 47.2 %copy-start.2 = (f32[512]{0:T(512)S(1)}, f32[512]{0:T(512)}, u32[]{:S(2)}) copy-start(f32[512]{0:T(512)} %param.6) | copy-start | bytes 6148
  6.5 47.2 %copy-start.1 = (f32[512]{0:T(512)S(1)}, f32[512]{0:T(512)}, u32[]{:S(2)}) copy-start(f32[512]{0:T(512)} %param.7) | copy-start | bytes 6148
  6.5 133.6 %all-gather.2.cloned.1.call-start = ((), (), s32[]{:S(2)}) async-start(), calls=%async_computation | async-start | bytes 15728640 | tf_op jit(solution)/shard_map/all_gather | solution.py:18
  53.7 86.4 %copy-start.3 = (f32[512]{0:T(512)S(1)}, f32[512]{0:T(512)}, u32[]{:S(2)}) copy-start(f32[512]{0:T(512)} %param.9) | copy-start | bytes 6148
Sparse Core Ops, SparseCore 0:
  59.3 80.8 all-gather.1
where the time goes:
time: 159 us; the launch traced here: 158 us
  waiting for transfers between devices  81 us (51%)
  blocking collectives  40.2 us (25%)
  between operations  13.4 us (8%)
  other arithmetic  12.3 us (8%)
  matrix products  11.3 us (7%)
    all_gather x1, waiting for transfers between devices, local(): lax.all_gather(normed, 'feat', axis=1, tiled=True)  81 us
    psum x1, blocking collectives, local(): sums = lax.psum(jnp.sum(features, axis=0), 'dp')  23.1 us
    psum x1, blocking collectives, local(): devs = lax.psum(jnp.sum(centred_here * centred_here, axis=0), 'dp')  17.1 us
    dot_general x1, matrix products, local(): jnp.dot(lax.all_gather(normed, 'feat', axis=1, tiled=True), weight, prefe...  11.3 us
    convert_element_type x1, other arithmetic, local(): normed = ((features - mean) * scale + beta).astype(jnp.bfloat16)  5.36 us
    reduce_sum x1, other arithmetic, local(): devs = lax.psum(jnp.sum(centred_here * centred_here, axis=0), 'dp')  3.52 us
    reduce_sum x1, other arithmetic, local(): sums = lax.psum(jnp.sum(features, axis=0), 'dp')  3.4 us
  transfers between devices with their start and end apart: 1, of which 1 were waited for; matrix products, arithmetic and copies ran while one was open for 0% of the time, Pallas kernels for 0%

commit v1 on v0

--- a/solution.py
+++ b/solution.py
@@ -10,7 +10,7 @@
     sums = lax.psum(jnp.sum(features, axis=0), "dp")
     mean = sums / total_rows
     centred_here = features - mean
-    devs = lax.psum(jnp.sum(centred_here * centred_here, axis=0), "dp")
+    devs = jnp.sum(lax.all_gather(jnp.sum(centred_here * centred_here, axis=0), "dp"), axis=0)
     var = devs / total_rows
     scale = gamma / jnp.sqrt(var + 1e-05)
     normed = ((features - mean) * scale + beta).astype(jnp.bfloat16)

time: 159 us -> 166 us (1.044)
  blocking collectives: 40.2 us -> 49.2 us
    all_gather x0 -> x1, blocking collectives: none -> 26.1 us  [local(): lax.all_gather(jnp.sum(centred_here * centred_here, axis=0), 'dp')]
    psum x1 -> x0, blocking collectives: 17.1 us -> none  [local(): devs = lax.psum(jnp.sum(centred_here * centred_here, axis=0), 'dp')]
    reduce_sum x1 -> x2, other arithmetic: 3.52 us -> 3.55 us  [the longest x1 3.52 us: local(): jnp.sum(centred_here * centred_here, axis=0)]
where the time goes in v1:
time: 166 us
  waiting for transfers between devices  79.5 us (48%)
  blocking collectives  49.2 us (30%)
  between operations  13.4 us (8%)
  other arithmetic  12.3 us (7%)
  matrix products  11.3 us (7%)
    all_gather x1, waiting for transfers between devices, local(): lax.all_gather(normed, 'feat', axis=1, tiled=True)  79.5 us
    all_gather x1, blocking collectives, local(): lax.all_gather(jnp.sum(centred_here * centred_here, axis=0), 'dp')  26.1 us
    psum x1, blocking collectives, local(): sums = lax.psum(jnp.sum(features, axis=0), 'dp')  23.1 us
    dot_general x1, matrix products, local(): jnp.dot(lax.all_gather(normed, 'feat', axis=1, tiled=True), weight, prefe...  11.3 us
    convert_element_type x1, other arithmetic, local(): normed = ((features - mean) * scale + beta).astype(jnp.bfloat16)  5.36 us
    reduce_sum x1, other arithmetic, local(): jnp.sum(centred_here * centred_here, axis=0)  3.52 us
    reduce_sum x1, other arithmetic, local(): sums = lax.psum(jnp.sum(features, axis=0), 'dp')  3.4 us
  transfers between devices with their start and end apart: 1, of which 1 were waited for; matrix products, arithmetic and copies ran while one was open for 0% of the time, Pallas kernels for 0%

profile of v1, /device:TPU:0, one launch (start us, length us, event | category | flops | bytes accessed | tf_op | source)
XLA Modules:
  0.0 165.9 jit_solution(11281098698904760288)
XLA Ops:
  6.5 0.0 copy-start
  6.5 0.0 copy-start.2
  6.5 0.0 copy-start.1
  6.5 0.0 all-gather.4.cloned.1.call-start
  6.5 3.4 %reduce_sum.27 = f32[512]{0:T(512)S(1)} reduce(f32[3072,512]{1,0:T(8,128)} %param.5, f32[]{:T(128)} %constant.3.clone.1), dimensions={0}, to_apply=%region_0.0 | reduce | flops 1572352 | bytes 6293508 | tf_op jit(solution)/shard_map/reduce_sum | solution.py:10
  9.9 23.1 %psum.7 = f32[512]{0:T(512)S(1)} all-reduce(f32[512]{0:T(512)S(1)} %reduce_sum.27), channel_id=1, replica_groups=mesh['dp'=8,'feat'=4] {'dp'}, use_global_device_ids=true, to_apply=%region_1.0 | all-reduce | flops 512 | bytes 4096 | tf_op jit(solution)/shard_map/psum | solution.py:10
  33.1 3.5 %multiply_reduce_fusion = f32[512]{0:T(512)S(1)} fusion(f32[3072,512]{1,0:T(8,128)} %param.5, f32[512]{0:T(512)S(1)} %broadcast_multiply_fusion), kind=kLoop, calls=%fused_computation.2 | loop fusion | flops 4718080 | bytes 6295552 | tf_op jit(solution)/shard_map/reduce_sum | solution.py:13
  36.6 26.1 %all-gather.1 = f32[8,1,512]{2,1,0:T(1,128)S(1)} all-gather(f32[1,1,512]{2,1,0:T(1,128)S(1)} %bitcast.3), channel_id=2, replica_groups=mesh['dp'=8,'feat'=4] {'dp'}, dimensions={0}, use_global_device_ids=true | all-gather | bytes 18432 | tf_op jit(solution)/shard_map/all_gather | solution.py:13
  62.7 0.0 copy-done.2
  62.8 0.0 copy-done.1
  62.8 0.0 copy-start.3
  62.8 5.4 %add_convert_fusion = bf16[3072,512]{1,0:T(8,128)(2,1)} fusion(f32[3072,512]{1,0:T(8,128)} %param.5, f32[512]{0:T(512)S(1)} %copy-done.1, f32[512]{0:T(512)S(1)} %rsqrt_multiply_fusion, f32[512]{0:T(512)S(1)} %broadcast_multiply_fusion), kind=kLoop, calls=%fused_computation.1 | loop fusion | flops 6291456 | bytes 9443328 | tf_op jit(solution)/shard_map/convert_element_type | solution.py:16
  68.1 0.0 all-gather.4.cloned.1.call-update
  68.2 79.5 %all-gather.4.cloned.1.call-done = bf16[3072,2048]{1,0:T(8,128)(2,1)} async-done(((bf16[3072,512]{1,0:T(8,128)(2,1)}), bf16[3072,2048]{1,0:T(8,128)(2,1)}) %all-gather.4.cloned.1.call-update) | async-done | bytes 12582928 | tf_op jit(solution)/shard_map/all_gather | solution.py:18
  147.7 0.0 copy-done
  147.7 0.0 copy-done.3
  147.7 11.3 %add_maximum_fusion = f32[3072,512]{1,0:T(8,128)} fusion(bf16[3072,2048]{1,0:T(8,128)(2,1)} %all-gather.4.cloned.1.call-done, bf16[2048,512]{1,0:T(8,128)(2,1)S(1)} %copy-done, f32[512]{0:T(512)S(1)} %copy-done.3), kind=kOutput, calls=%fused_computation | convolution fusion | flops 6445596672 | bytes 20973568 | tf_op jit(solution)/shard_map/dot_general | solution.py:17
  (3 shorter events, 0.0 us)
Async XLA Ops:
  6.5 141.2 %copy-start = (bf16[2048,512]{1,0:T(8,128)(2,1)S(1)}, bf16[2048,512]{1,0:T(8,128)(2,1)}, u32[]{:S(2)}) copy-start(bf16[2048,512]{1,0:T(8,128)(2,1)} %param.8) | copy-start | bytes 6291460
  6.5 56.2 %copy-start.2 = (f32[512]{0:T(512)S(1)}, f32[512]{0:T(512)}, u32[]{:S(2)}) copy-start(f32[512]{0:T(512)} %param.6) | copy-start | bytes 6148
  6.5 56.2 %copy-start.1 = (f32[512]{0:T(512)S(1)}, f32[512]{0:T(512)}, u32[]{:S(2)}) copy-start(f32[512]{0:T(512)} %param.7) | copy-start | bytes 6148
  6.5 141.1 %all-gather.4.cloned.1.call-start = ((), (), s32[]{:S(2)}) async-start(), calls=%async_computation | async-start | bytes 15728640 | tf_op jit(solution)/shard_map/all_gather | solution.py:18
  62.8 84.9 %copy-start.3 = (f32[512]{0:T(512)S(1)}, f32[512]{0:T(512)}, u32[]{:S(2)}) copy-start(f32[512]{0:T(512)} %param.9) | copy-start | bytes 6148
Sparse Core Ops, SparseCore 0:
  68.3 79.3 all-gather.3
